TPU v7x, 32 devices: a whole 2x2x4 slice. The times are simulated.
32 devices in a mesh: ep: 4 (over y, core), etp: 8 (over z, x).
Axes of the slice: x: 2, y: 2, z: 4, core: 2. Of those that a mesh axis runs over, the one named last changes fastest.
Arguments:
- tokens: bfloat16 [4096, 7168], P(('ep', 'etp')), may hold values from -6 to 6
- expert_ids: int32 [4096, 8], P(('ep', 'etp')), may hold values from 0 to 383, all different within a row; in each aligned block of 128 rows (0 to 127, 128 to 255, ...) at most 3 rows name the same one
- gate_q: int32 [4096, 8], P(('ep', 'etp')), may hold values from 1 to 1024
- w_gate: bfloat16 [4, 7168, 2048], P('ep', None, 'etp'), may hold values from -0.0625 to 0.0625
- w_up: bfloat16 [4, 7168, 2048], P('ep', None, 'etp'), may hold values from -0.0625 to 0.0625
- w_down: bfloat16 [4, 2048, 7168], P('ep', 'etp'), may hold values from -0.125 to 0.125
Outputs:
- mixed: bfloat16 [4096, 7168], P(('ep', 'etp'))
Inputs may be any that keep to these rules, and one draw needn't show every extreme that they name: `expert_ids`: each row names 8 different experts; among the 128 rows of one device no expert is named by more than 3 rows.
All inputs are finite; a program needn't handle non-finite values.
Results may differ from a plain program's by a relative error of at most 0.014.
Values may be sent and summed in bfloat16 or wider, within the bound.
A program may use at most 64 MiB of HBM per device.

v0:
```python
import jax
import jax.numpy as jnp
from jax import lax
from jax.sharding import PartitionSpec as P

CAP = 3


def body(tokens, expert_ids, gate_q, w_gate, w_up, w_down):
    groups = lax.axis_size("ep")
    members = lax.axis_size("etp")
    capacity = CAP
    width = tokens.shape[1]
    count_rows = tokens.shape[0]
    flat_ids = expert_ids.reshape(-1)
    owner_hot = (flat_ids[:, None] == jnp.arange(groups, dtype=jnp.int32)[None, :]).astype(
        jnp.int32
    )
    earlier = jnp.cumsum(owner_hot, axis=0) - owner_hot
    position = jnp.sum(earlier * owner_hot, axis=1)
    column = jnp.where(flat_ids < groups, flat_ids * capacity + position, -1)
    select = (column[:, None] == jnp.arange(groups * capacity, dtype=jnp.int32)[None, :]).astype(
        jnp.float32
    )
    select = select.reshape(count_rows, -1, groups * capacity)
    placing = jnp.sum(select, axis=1)
    gate_scale = gate_q.astype(jnp.float32) / 1024.0
    scaling = jnp.sum(select * gate_scale[:, :, None], axis=1)
    bucket = jnp.einsum(
        "tc,td->cd", placing.astype(jnp.bfloat16), tokens, preferred_element_type=jnp.float32
    )
    bucket = bucket.astype(jnp.bfloat16).reshape(groups, capacity, width)
    gathered = lax.all_gather(bucket, "etp", axis=1, tiled=True)
    arrived = lax.all_to_all(gathered, "ep", split_axis=0, concat_axis=0, tiled=True)
    gate = jnp.dot(arrived, w_gate[0], preferred_element_type=jnp.float32)
    upper = jnp.dot(arrived, w_up[0], preferred_element_type=jnp.float32)
    hidden = (jax.nn.silu(gate) * upper).astype(jnp.bfloat16)
    inner = hidden.shape[2]
    ordered = (
        hidden.reshape(groups, members, capacity, inner).transpose(1, 0, 2, 3).reshape(-1, inner)
    )
    term = jnp.dot(ordered, w_down[0], preferred_element_type=jnp.float32)
    rounded = lax.optimization_barrier(term.astype(jnp.bfloat16))
    summed = lax.psum_scatter(
        rounded.astype(jnp.float32).astype(jnp.bfloat16), "etp", scatter_dimension=0, tiled=True
    )
    local_out = summed.reshape(groups, capacity, width)
    results = lax.all_to_all(local_out, "ep", split_axis=0, concat_axis=0, tiled=True)
    flat_out = results.reshape(groups * capacity, width).astype(jnp.float32)
    mixed = jnp.dot(scaling, flat_out, precision=lax.Precision.HIGHEST)
    return mixed.astype(jnp.bfloat16)


def solution(mesh):
    in_specs = (
        P(("ep", "etp"), None),
        P(("ep", "etp"), None),
        P(("ep", "etp"), None),
        P("ep", None, "etp"),
        P("ep", None, "etp"),
        P("ep", "etp", None),
    )
    out_specs = P(("ep", "etp"), None)
    return jax.shard_map(body, mesh=mesh, in_specs=in_specs, out_specs=out_specs, check_vma=False)
```

profile of v0, /device:TPU:0, one launch (start us, length us, event | category | flops | bytes accessed | tf_op | source)
XLA Modules:
  0.0 157.0 jit_solution(10917868213449177721)
XLA Ops:
  6.5 0.9 copy.40
  7.7 1.1 reduce-window.6
  8.8 0.2 slice_reduce_fusion
  9.0 0.2 reduce-window.9
  9.4 0.7 add_select_fusion
  10.2 0.7 convert_multiply_fusion
  10.9 0.3 convolution_convert_fusion.2
  11.4 0.8 copy.43
  12.2 45.0 %all-gather.2.cloned.1.call-done = bf16[4,24,7168]{2,0,1:T(4,128)(2,1)} async-done(((bf16[4,3,7168]{2,0,1:T(4,128)(2,1)}), bf16[4,24,7168]{2,0,1:T(4,128)(2,1)}) %all-gather.2.cloned.1.call-update) | async-done | bytes 1376272 | tf_op jit(solution)/shard_map/all_gather | solution.py:33
  57.2 1.9 %copy.44 = bf16[4,24,7168]{2,1,0:T(8,128)(2,1)S(1)} copy(bf16[4,24,7168]{2,0,1:T(4,128)(2,1)} %all-gather.2.cloned.1.call-done) | data formatting | bytes 2752512 | tf_op jit(solution)/shard_map/all_gather | solution.py:33
  59.1 20.5 %all_to_all.10 = bf16[4,24,7168]{2,1,0:T(8,128)(2,1)S(1)} all-to-all(bf16[4,24,7168]{2,1,0:T(8,128)(2,1)S(1)} %copy.44), channel_id=1, replica_groups=mesh['ep'=4,'etp'=8] {'ep'}, dimensions={0} | all-to-all | bytes 2752512 | tf_op jit(solution)/shard_map/all_to_all | solution.py:34
  79.6 0.7 fusion.4
  80.3 1.3 copy-done.2
  81.6 0.7 fusion.9
  82.5 2.8 %convolution_convert_fusion.1 = bf16[96,7168]{1,0:T(8,128)(2,1)S(1)} fusion(bf16[96,256]{1,0:T(8,128)(2,1)S(1)} %reshape.58, bf16[1,256,7168]{2,1,0:T(8,128)(2,1)} %param.11), kind=kOutput, calls=%fused_computation.1 | convolution fusion | flops 353009664 | bytes 5095424 | tf_op jit(solution)/shard_map/dot_general | solution.py:42
  85.3 43.2 %fusion = bf16[16,7168]{1,0:T(8,128)(2,1)S(1)} fusion(bf16[96,7168]{1,0:T(8,128)(2,1)S(1)} %convolution_convert_fusion.1), kind=kCustom, calls=%all-reduce-scatter | all-reduce-scatter fusion | flops 917505 | bytes 1606144
  128.5 1.5 collective-permute-start
  130.1 4.1 %collective-permute-start.1 = (bf16[12,7168]{1,0:T(8,128)(2,1)S(1)}, bf16[12,7168]{1,0:T(8,128)(2,1)S(1)}, u32[]{:S(2)}, u32[]{:S(2)}) collective-permute-start(bf16[12,7168]{1,0:T(8,128)(2,1)S(1)} %slice.9), channel_id=1, source_target_pairs={{0,2},{1,3},{2,4},{3,5},{4,6},{5,7},{8,10},{9,11},{10,12},{11,13},... | collective-permute-start | bytes 516104
  134.2 0.6 dynamic-slice.4
  135.4 2.3 %collective-permute-done.1 = bf16[12,7168]{1,0:T(8,128)(2,1)S(1)} collective-permute-done((bf16[12,7168]{1,0:T(8,128)(2,1)S(1)}, bf16[12,7168]{1,0:T(8,128)(2,1)S(1)}, u32[]{:S(2)}, u32[]{:S(2)}) %collective-permute-start.1) | collective-permute-done | bytes 172064
  137.7 1.2 concatenate
  139.1 8.0 %all_to_all.11 = bf16[4,3,7168]{2,1,0:T(4,128)(2,1)S(1)} all-to-all(bf16[4,3,7168]{2,1,0:T(4,128)(2,1)S(1)} %reshape.59), channel_id=1, replica_groups=mesh['ep'=4,'etp'=8] {'ep'}, dimensions={0} | all-to-all | bytes 344064 | tf_op jit(solution)/shard_map/all_to_all | solution.py:48
  147.1 0.2 reshape.60
  147.3 2.9 %convolution_convert_fusion = bf16[128,7168]{1,0:T(8,128)(2,1)} fusion(f32[128,12]{0,1:T(8,128)S(1)} %get-tuple-element.6, bf16[12,7168]{1,0:T(8,128)(2,1)S(1)} %reshape.60), kind=kOutput, calls=%fused_computation | convolution fusion | flops 133038080 | bytes 2013184 | tf_op jit(solution)/shard_map/dot_general | solution.py:50
  (25 shorter events, 1.0 us)
Async XLA Ops:
  6.5 4.4 %copy-start = (bf16[128,7168]{1,0:T(8,128)(2,1)S(1)}, bf16[128,7168]{1,0:T(8,128)(2,1)}, u32[]{:S(2)}) copy-start(bf16[128,7168]{1,0:T(8,128)(2,1)} %param.6) | copy-start | bytes 5505028
  6.5 50.7 %all-gather.2.cloned.1.call-start = ((), (), s32[]{:S(2)}) async-start(), calls=%async_computation.2 | async-start | bytes 1548288 | tf_op jit(solution)/shard_map/all_gather | solution.py:33
  57.2 22.4 %copy-start.1 = (bf16[1,7168,256]{2,1,0:T(8,128)(2,1)S(1)}, bf16[1,7168,256]{2,1,0:T(8,128)(2,1)}, u32[]{:S(2)}) copy-start(bf16[1,7168,256]{2,1,0:T(8,128)(2,1)} %param.9) | copy-start | bytes 11010052
  79.6 2.0 %copy-start.2 = (bf16[1,7168,256]{2,1,0:T(8,128)(2,1)S(1)}, bf16[1,7168,256]{2,1,0:T(8,128)(2,1)}, u32[]{:S(2)}) copy-start(bf16[1,7168,256]{2,1,0:T(8,128)(2,1)} %param.10) | copy-start | bytes 11010052
  85.2 48.9 %copy-start.3 = (u32[32]{0:T(128)S(1)}, u32[32]{0:T(128)}, u32[]{:S(2)}) copy-start(u32[32]{0:T(128)} %constant.26) | copy-start | bytes 388
  128.5 9.2 %collective-permute-start = (bf16[16,7168]{1,0:T(8,128)(2,1)S(1)}, bf16[16,7168]{1,0:T(8,128)(2,1)S(1)}, u32[]{:S(2)}, u32[]{:S(2)}) collective-permute-start(bf16[16,7168]{1,0:T(8,128)(2,1)S(1)} %fusion), channel_id=1, source_target_pairs={{0,1},{1,2},{2,3},{3,4},{4,5},{5,6},{6,7},{8,9},{9,10},{10,11},{11... | collective-permute-start | bytes 688136
  130.1 7.6 %collective-permute-start.1 = (bf16[12,7168]{1,0:T(8,128)(2,1)S(1)}, bf16[12,7168]{1,0:T(8,128)(2,1)S(1)}, u32[]{:S(2)}, u32[]{:S(2)}) collective-permute-start(bf16[12,7168]{1,0:T(8,128)(2,1)S(1)} %slice.9), channel_id=1, source_target_pairs={{0,2},{1,3},{2,4},{3,5},{4,6},{5,7},{8,10},{9,11},{10,12},{11,13},... | collective-permute-start | bytes 516104
Sparse Core Ops, SparseCore 0:
  12.3 44.8 all-gather.1
where the time goes:
time: 157 us
  blocking collectives  71.8 us (46%)
  waiting for transfers between devices  47.3 us (30%)
  between operations  14.2 us (9%)
  local copies, waits for them, and re-layouts  7.82 us (5%)
  matrix products  7.42 us (5%)
  starting transfers between devices  5.6 us (4%)
  other arithmetic  2.87 us (2%)
    all_gather x1, waiting for transfers between devices, body(): gathered = lax.all_gather(bucket, 'etp', axis=1, tiled=True)  45 us
    unnamed x1, blocking collectives  43.2 us
    all_to_all x1, blocking collectives, body(): lax.all_to_all(gathered, 'ep', split_axis=0, concat_axis=0, tiled=True)  20.5 us
    all_to_all x1, blocking collectives, body(): lax.all_to_all(local_out, 'ep', split_axis=0, concat_axis=0, tiled=True)  8.03 us
    unnamed x2, starting transfers between devices  5.6 us
    unnamed x13, local copies, waits for them, and re-layouts  4.14 us
  transfers between devices with their start and end apart: 3, of which 2 were waited for; matrix products, arithmetic and copies ran while one was open for 0% of the time, Pallas kernels for 0%

commit v1 on v0

--- a/solution.py
+++ b/solution.py
@@ -1,9 +1,30 @@
+import functools
 import jax
 import jax.numpy as jnp
 from jax import lax
 from jax.sharding import PartitionSpec as P
 
 CAP = 3
+
+
+def register_grid_over_axis(incoming_x, which_axis):
+    size_here = lax.axis_size(which_axis)
+    made = tuple(((q, (q + 1) % size_here) for q in range(size_here)))
+    found = tuple(((q, (q - 1) % size_here) for q in range(size_here)))
+    a_next, kept_arr = ([incoming_x], [incoming_x])
+    for _ in range(size_here // 2):
+        a_next.append(lax.ppermute(a_next[-1], which_axis, made))
+    for _ in [*range((size_here - 1) // 2)]:
+        kept_arr.append(lax.ppermute(kept_arr[-1], which_axis, found))
+    work_now = jnp.roll(
+        jnp.concatenate([*a_next[::-1], *kept_arr[1:]], axis=1),
+        (lax.axis_index(which_axis) - size_here // 2) * incoming_x.shape[1],
+        1,
+    )
+    return work_now
+
+
+clear_patch = functools.partial(register_grid_over_axis, which_axis="etp")
 
 
 def body(tokens, expert_ids, gate_q, w_gate, w_up, w_down):
@@ -30,7 +51,7 @@
         "tc,td->cd", placing.astype(jnp.bfloat16), tokens, preferred_element_type=jnp.float32
     )
     bucket = bucket.astype(jnp.bfloat16).reshape(groups, capacity, width)
-    gathered = lax.all_gather(bucket, "etp", axis=1, tiled=True)
+    gathered = clear_patch(bucket)
     arrived = lax.all_to_all(gathered, "ep", split_axis=0, concat_axis=0, tiled=True)
     gate = jnp.dot(arrived, w_gate[0], preferred_element_type=jnp.float32)
     upper = jnp.dot(arrived, w_up[0], preferred_element_type=jnp.float32)

time: 157 us -> 201 us (1.28)
  the two profiles are of different devices: /device:TPU:0 before, /device:TPU:26 now
where the time goes in v1:
time: 201 us; the launch traced here: 198 us
  blocking collectives  71.1 us (35%)
  local copies, waits for them, and re-layouts  62.2 us (31%)
  waiting for transfers between devices  44.7 us (22%)
  starting transfers between devices  8.71 us (4%)
  matrix products  7.43 us (4%)
  other arithmetic  2.87 us (1%)
    concatenate x1, local copies, waits for them, and re-layouts, register_grid_over_axis(): jnp.roll(jnp.concatenate([*a_next[::-1], *kept_arr[1:]], axis=1), (lax.ax...  55.1 us
    unnamed x1, blocking collectives  42.5 us
    ppermute x4, waiting for transfers between devices, register_grid_over_axis(): a_next.append(lax.ppermute(a_next[-1], which_axis, made))  36.9 us
    all_to_all x1, blocking collectives, body(): lax.all_to_all(gathered, 'ep', split_axis=0, concat_axis=0, tiled=True)  20.5 us
    all_to_all x1, blocking collectives, body(): lax.all_to_all(local_out, 'ep', split_axis=0, concat_axis=0, tiled=True)  8.03 us
    unnamed x2, waiting for transfers between devices  7.88 us
    ppermute x3, starting transfers between devices, register_grid_over_axis(): kept_arr.append(lax.ppermute(kept_arr[-1], which_axis, found))  6.06 us
    unnamed x13, local copies, waits for them, and re-layouts  4.14 us
  transfers between devices with their start and end apart: 9, of which 5 were waited for; matrix products, arithmetic and copies ran while one was open for 0% of the time, Pallas kernels for 0%

profile of v1, /device:TPU:26, one launch (start us, length us, event | category | flops | bytes accessed | tf_op | source)
XLA Modules:
  0.0 197.9 jit_solution(9229403574446773840)
XLA Ops:
  0.0 0.9 copy.36
  1.1 1.1 reduce-window.6
  2.9 0.7 add_select_fusion
  4.9 2.0 %collective-permute-start.4 = (bf16[4,3,7168]{2,1,0:T(4,128)(2,1)S(1)}, bf16[4,3,7168]{2,1,0:T(4,128)(2,1)S(1)}, u32[]{:S(2)}, u32[]{:S(2)}) collective-permute-start(bf16[4,3,7168]{2,1,0:T(4,128)(2,1)S(1)} %reshape.56), channel_id=1, source_target_pairs={{0,7},{1,0},{2,1},{3,2},{4,3},{5,4},{6,5},{7,6},{8,15},{9,8},{10,9... | collective-permute-start | bytes 516104 | tf_op jit(solution)/shard_map/ppermute | solution.py:18
  6.9 10.2 %collective-permute-done = bf16[4,3,7168]{2,1,0:T(4,128)(2,1)S(1)} collective-permute-done((bf16[4,3,7168]{2,1,0:T(4,128)(2,1)S(1)}, bf16[4,3,7168]{2,1,0:T(4,128)(2,1)S(1)}, u32[]{:S(2)}, u32[]{:S(2)}) %collective-permute-start) | collective-permute-done | bytes 172064 | tf_op jit(solution)/shard_map/ppermute | solution.py:16
  17.2 2.0 %collective-permute-start.5 = (bf16[4,3,7168]{2,1,0:T(4,128)(2,1)S(1)}, bf16[4,3,7168]{2,1,0:T(4,128)(2,1)S(1)}, u32[]{:S(2)}, u32[]{:S(2)}) collective-permute-start(bf16[4,3,7168]{2,1,0:T(4,128)(2,1)S(1)} %collective-permute-done.4), channel_id=1, source_target_pairs={{0,7},{1,0},{2,1},{3,2},{4,3},{5,4},{6,5},{7,6},{8,15},{9,8},{10,9... | collective-permute-start | bytes 516104 | tf_op jit(solution)/shard_map/ppermute | solution.py:18
  19.2 9.4 %collective-permute-done.1 = bf16[4,3,7168]{2,1,0:T(4,128)(2,1)S(1)} collective-permute-done((bf16[4,3,7168]{2,1,0:T(4,128)(2,1)S(1)}, bf16[4,3,7168]{2,1,0:T(4,128)(2,1)S(1)}, u32[]{:S(2)}, u32[]{:S(2)}) %collective-permute-start.1) | collective-permute-done | bytes 172064 | tf_op jit(solution)/shard_map/ppermute | solution.py:16
  28.6 2.0 %collective-permute-start.6 = (bf16[4,3,7168]{2,1,0:T(4,128)(2,1)S(1)}, bf16[4,3,7168]{2,1,0:T(4,128)(2,1)S(1)}, u32[]{:S(2)}, u32[]{:S(2)}) collective-permute-start(bf16[4,3,7168]{2,1,0:T(4,128)(2,1)S(1)} %collective-permute-done.5), channel_id=1, source_target_pairs={{0,7},{1,0},{2,1},{3,2},{4,3},{5,4},{6,5},{7,6},{8,15},{9,8},{10,9... | collective-permute-start | bytes 516104 | tf_op jit(solution)/shard_map/ppermute | solution.py:18
  30.6 11.1 %collective-permute-done.2 = bf16[4,3,7168]{2,1,0:T(4,128)(2,1)S(1)} collective-permute-done((bf16[4,3,7168]{2,1,0:T(4,128)(2,1)S(1)}, bf16[4,3,7168]{2,1,0:T(4,128)(2,1)S(1)}, u32[]{:S(2)}, u32[]{:S(2)}) %collective-permute-start.2) | collective-permute-done | bytes 172064 | tf_op jit(solution)/shard_map/ppermute | solution.py:16
  41.7 6.1 %collective-permute-done.3 = bf16[4,3,7168]{2,1,0:T(4,128)(2,1)} collective-permute-done((bf16[4,3,7168]{2,1,0:T(4,128)(2,1)S(1)}, bf16[4,3,7168]{2,1,0:T(4,128)(2,1)}, u32[]{:S(2)}, u32[]{:S(2)}) %collective-permute-start.3) | collective-permute-done | bytes 172064 | tf_op jit(solution)/shard_map/ppermute | solution.py:16
  47.8 55.1 %concatenate.6 = bf16[4,48,7168]{2,1,0:T(8,128)(2,1)} concatenate(bf16[4,3,7168]{2,1,0:T(4,128)(2,1)} %collective-permute-done.3, bf16[4,3,7168]{2,1,0:T(4,128)(2,1)S(1)} %collective-permute-done.2, bf16[4,3,7168]{2,1,0:T(4,128)(2,1)S(1)} %collective-permute-done.1, bf16[4,3,7168]{2,1,0:T(4,128)(2,1)S(1)} %collective-permute-done, bf16[4,3,7168]{2,1,0:T(4,128)(2,1)S(1)} %reshape.56, ...), dimensions={1} | concatenate | bytes 5505024 | tf_op jit(solution)/shard_map/jit(_roll_dynamic)/concatenate | solution.py:19
  102.9 2.0 %constant_dynamic-slice_fusion.1 = bf16[4,24,7168]{2,1,0:T(8,128)(2,1)S(1)} fusion(bf16[4,48,7168]{2,1,0:T(8,128)(2,1)} %concatenate.6, s32[]{:T(128)S(6)} %select_n.23), kind=kLoop, calls=%fused_computation.25 | loop fusion | bytes 2752516 | tf_op jit(solution)/shard_map/jit(_roll_dynamic)/dynamic_slice | solution.py:19
  104.9 20.5 %all_to_all.10 = bf16[4,24,7168]{2,1,0:T(8,128)(2,1)S(1)} all-to-all(bf16[4,24,7168]{2,1,0:T(8,128)(2,1)S(1)} %constant_dynamic-slice_fusion.1), channel_id=1, replica_groups=mesh['ep'=4,'etp'=8] {'ep'}, dimensions={0} | all-to-all | bytes 2752512 | tf_op jit(solution)/shard_map/all_to_all | solution.py:55
  125.5 0.7 fusion.4
  126.2 1.3 copy-done.2
  127.5 0.7 multiply_convert_fusion
  128.4 2.8 %convolution_convert_fusion.1 = bf16[96,7168]{1,0:T(8,128)(2,1)S(1)} fusion(bf16[96,256]{1,0:T(8,128)(2,1)S(1)} %reshape.58, bf16[1,256,7168]{2,1,0:T(8,128)(2,1)} %param.11), kind=kOutput, calls=%fused_computation.1 | convolution fusion | flops 353009664 | bytes 5095424 | tf_op jit(solution)/shard_map/dot_general | solution.py:63
  131.1 42.5 %fusion = bf16[16,7168]{1,0:T(8,128)(2,1)S(1)} fusion(bf16[96,7168]{1,0:T(8,128)(2,1)S(1)} %convolution_convert_fusion.1), kind=kCustom, calls=%all-reduce-scatter | all-reduce-scatter fusion | flops 917505 | bytes 1606144
  173.6 1.3 collective-permute-start.7
  175.0 1.3 collective-permute-start.8
  177.5 7.9 %collective-permute-done.8 = bf16[12,7168]{1,0:T(8,128)(2,1)S(1)} collective-permute-done((bf16[12,7168]{1,0:T(8,128)(2,1)S(1)}, bf16[12,7168]{1,0:T(8,128)(2,1)S(1)}, u32[]{:S(2)}, u32[]{:S(2)}) %collective-permute-start.8) | collective-permute-done | bytes 172064
  185.4 1.2 concatenate.7
  186.8 8.0 %all_to_all.11 = bf16[4,3,7168]{2,1,0:T(4,128)(2,1)S(1)} all-to-all(bf16[4,3,7168]{2,1,0:T(4,128)(2,1)S(1)} %reshape.59), channel_id=1, replica_groups=mesh['ep'=4,'etp'=8] {'ep'}, dimensions={0} | all-to-all | bytes 344064 | tf_op jit(solution)/shard_map/all_to_all | solution.py:69
  195.0 2.9 %convolution_convert_fusion = bf16[128,7168]{1,0:T(8,128)(2,1)} fusion(f32[128,12]{0,1:T(8,128)S(1)} %get-tuple-element.6, bf16[12,7168]{1,0:T(8,128)(2,1)S(1)} %reshape.60), kind=kOutput, calls=%fused_computation | convolution fusion | flops 133038080 | bytes 2013184 | tf_op jit(solution)/shard_map/dot_general | solution.py:71
  (36 shorter events, 3.2 us)
Async XLA Ops:
  0.0 4.4 %copy-start = (bf16[128,7168]{1,0:T(8,128)(2,1)S(1)}, bf16[128,7168]{1,0:T(8,128)(2,1)}, u32[]{:S(2)}) copy-start(bf16[128,7168]{1,0:T(8,128)(2,1)} %param.6) | copy-start | bytes 5505028
  4.8 12.3 %collective-permute-start = (bf16[4,3,7168]{2,1,0:T(4,128)(2,1)S(1)}, bf16[4,3,7168]{2,1,0:T(4,128)(2,1)S(1)}, u32[]{:S(2)}, u32[]{:S(2)}) collective-permute-start(bf16[4,3,7168]{2,1,0:T(4,128)(2,1)S(1)} %reshape.56), channel_id=1, source_target_pairs={{0,1},{1,2},{2,3},{3,4},{4,5},{5,6},{6,7},{7,0},{8,9},{9,10},{10,1... | collective-permute-start | bytes 516104 | tf_op jit(solution)/shard_map/ppermute | solution.py:16
  4.9 12.3 %collective-permute-start.4 = (bf16[4,3,7168]{2,1,0:T(4,128)(2,1)S(1)}, bf16[4,3,7168]{2,1,0:T(4,128)(2,1)S(1)}, u32[]{:S(2)}, u32[]{:S(2)}) collective-permute-start(bf16[4,3,7168]{2,1,0:T(4,128)(2,1)S(1)} %reshape.56), channel_id=1, source_target_pairs={{0,7},{1,0},{2,1},{3,2},{4,3},{5,4},{6,5},{7,6},{8,15},{9,8},{10,9... | collective-permute-start | bytes 516104 | tf_op jit(solution)/shard_map/ppermute | solution.py:18
  17.2 11.4 %collective-permute-start.1 = (bf16[4,3,7168]{2,1,0:T(4,128)(2,1)S(1)}, bf16[4,3,7168]{2,1,0:T(4,128)(2,1)S(1)}, u32[]{:S(2)}, u32[]{:S(2)}) collective-permute-start(bf16[4,3,7168]{2,1,0:T(4,128)(2,1)S(1)} %collective-permute-done), channel_id=1, source_target_pairs={{0,1},{1,2},{2,3},{3,4},{4,5},{5,6},{6,7},{7,0},{8,9},{9,10},{10,1... | collective-permute-start | bytes 516104 | tf_op jit(solution)/shard_map/ppermute | solution.py:16
  17.2 11.4 %collective-permute-start.5 = (bf16[4,3,7168]{2,1,0:T(4,128)(2,1)S(1)}, bf16[4,3,7168]{2,1,0:T(4,128)(2,1)S(1)}, u32[]{:S(2)}, u32[]{:S(2)}) collective-permute-start(bf16[4,3,7168]{2,1,0:T(4,128)(2,1)S(1)} %collective-permute-done.4), channel_id=1, source_target_pairs={{0,7},{1,0},{2,1},{3,2},{4,3},{5,4},{6,5},{7,6},{8,15},{9,8},{10,9... | collective-permute-start | bytes 516104 | tf_op jit(solution)/shard_map/ppermute | solution.py:18
  28.6 13.2 %collective-permute-start.2 = (bf16[4,3,7168]{2,1,0:T(4,128)(2,1)S(1)}, bf16[4,3,7168]{2,1,0:T(4,128)(2,1)S(1)}, u32[]{:S(2)}, u32[]{:S(2)}) collective-permute-start(bf16[4,3,7168]{2,1,0:T(4,128)(2,1)S(1)} %collective-permute-done.1), channel_id=1, source_target_pairs={{0,1},{1,2},{2,3},{3,4},{4,5},{5,6},{6,7},{7,0},{8,9},{9,10},{10,1... | collective-permute-start | bytes 516104 | tf_op jit(solution)/shard_map/ppermute | solution.py:16
  28.6 13.2 %collective-permute-start.6 = (bf16[4,3,7168]{2,1,0:T(4,128)(2,1)S(1)}, bf16[4,3,7168]{2,1,0:T(4,128)(2,1)S(1)}, u32[]{:S(2)}, u32[]{:S(2)}) collective-permute-start(bf16[4,3,7168]{2,1,0:T(4,128)(2,1)S(1)} %collective-permute-done.5), channel_id=1, source_target_pairs={{0,7},{1,0},{2,1},{3,2},{4,3},{5,4},{6,5},{7,6},{8,15},{9,8},{10,9... | collective-permute-start | bytes 516104 | tf_op jit(solution)/shard_map/ppermute | solution.py:18
  41.7 6.1 %collective-permute-start.3 = (bf16[4,3,7168]{2,1,0:T(4,128)(2,1)S(1)}, bf16[4,3,7168]{2,1,0:T(4,128)(2,1)}, u32[]{:S(2)}, u32[]{:S(2)}) collective-permute-start(bf16[4,3,7168]{2,1,0:T(4,128)(2,1)S(1)} %collective-permute-done.2), channel_id=1, source_target_pairs={{0,1},{1,2},{2,3},{3,4},{4,5},{5,6},{6,7},{7,0},{8,9},{9,10},{10,1... | collective-permute-start | bytes 516104 | tf_op jit(solution)/shard_map/ppermute | solution.py:16
  102.9 22.6 %copy-start.1 = (bf16[1,7168,256]{2,1,0:T(8,128)(2,1)S(1)}, bf16[1,7168,256]{2,1,0:T(8,128)(2,1)}, u32[]{:S(2)}) copy-start(bf16[1,7168,256]{2,1,0:T(8,128)(2,1)} %param.9) | copy-start | bytes 11010052
  125.5 2.0 %copy-start.2 = (bf16[1,7168,256]{2,1,0:T(8,128)(2,1)S(1)}, bf16[1,7168,256]{2,1,0:T(8,128)(2,1)}, u32[]{:S(2)}) copy-start(bf16[1,7168,256]{2,1,0:T(8,128)(2,1)} %param.10) | copy-start | bytes 11010052
  131.1 45.2 %copy-start.3 = (u32[32]{0:T(128)S(1)}, u32[32]{0:T(128)}, u32[]{:S(2)}) copy-start(u32[32]{0:T(128)} %constant.52) | copy-start | bytes 388
  173.6 11.8 %collective-permute-start.7 = (bf16[16,7168]{1,0:T(8,128)(2,1)S(1)}, bf16[16,7168]{1,0:T(8,128)(2,1)S(1)}, u32[]{:S(2)}, u32[]{:S(2)}) collective-permute-start(bf16[16,7168]{1,0:T(8,128)(2,1)S(1)} %fusion), channel_id=1, source_target_pairs={{0,1},{1,2},{2,3},{3,4},{4,5},{5,6},{6,7},{8,9},{9,10},{10,11},{11... | collective-permute-start | bytes 688136
  175.0 10.4 %collective-permute-start.8 = (bf16[12,7168]{1,0:T(8,128)(2,1)S(1)}, bf16[12,7168]{1,0:T(8,128)(2,1)S(1)}, u32[]{:S(2)}, u32[]{:S(2)}) collective-permute-start(bf16[12,7168]{1,0:T(8,128)(2,1)S(1)} %slice.9), channel_id=1, source_target_pairs={{0,2},{1,3},{2,4},{3,5},{4,6},{5,7},{8,10},{9,11},{10,12},{11,13},... | collective-permute-start | bytes 516104
